TPU v7x, 128 devices: a whole 4x4x4 slice. The times are simulated.
128 devices in a mesh: tp: 1, cp: 128 (over z, y, x, core).
Axes of the slice: x: 4, y: 4, z: 4, core: 2. Of those that a mesh axis runs over, the one named last changes fastest.
Arguments:
- query: bfloat16 [6, 1024, 16, 128], P(None, 'cp', 'tp')
- out_act: bfloat16 [6, 1024, 16, 128], P(None, 'cp', 'tp')
- out_grad: bfloat16 [6, 1024, 16, 128], P(None, 'cp', 'tp')
- row_lse: float32 [6, 1024, 16], P(None, 'cp', 'tp')
- key_act: bfloat16 [38912, 1, 128], P('cp', 'tp')
- value_act: bfloat16 [38912, 1, 128], P('cp', 'tp')
- doc_ids: int32 [38912], replicated
Outputs:
- output 1: bfloat16 [6, 1024, 16, 128], P(None, 'cp', 'tp')
- output 2: float32 [38912, 1, 128], P('cp', 'tp')
- output 3: float32 [38912, 1, 128], P('cp', 'tp')
All inputs are finite; a program needn't handle non-finite values.
Results may differ from a plain program's by a relative error of at most 0.001.
Values are sent between devices in bfloat16 or wider.
A program may use at most 1 GiB of HBM per device.

v0:
```python
import functools

import jax
import jax.numpy as jnp
from jax import lax
from jax.experimental import pallas as pl
from jax.experimental.pallas import tpu as pltpu
from jax.sharding import PartitionSpec as P

MESH = pl.DeviceIdType.MESH
TK = 256
LANES = 128
LOG2E = 1.4426950408889634
F32, BF16 = jnp.float32, jnp.bfloat16


def place():
    me = lax.axis_index('cp')
    return me // 32, lax.rem(me // 8, 4), lax.rem(me // 2, 4), lax.rem(me, 2)


def at(z, y, x, c):
    return ((z * 4 + y) * 4 + x) * 2 + c


def up(v):
    return lax.rem(v + 1, 4)


def down(v):
    return lax.rem(v + 3, 4)


def far(v):
    return lax.rem(v + 2, 4)


class Wire:
    def __init__(self, ssem, rsem):
        self.ssem, self.rsem, self.n, self.sent = ssem, rsem, 0, []

    def copy(self, src, dst, dev):
        cp = pltpu.make_async_remote_copy(
            src_ref=src, dst_ref=dst, send_sem=self.ssem.at[self.n], recv_sem=self.rsem.at[self.n],
            device_id={'cp': dev}, device_id_type=MESH)
        self.n += 1
        return cp

    def send(self, src, dst, dev):
        cp = self.copy(src, dst, dev)
        cp.start()
        self.sent.append(cp)
        return cp

    def finish(self):
        for cp in self.sent:
            cp.wait_send()


def greet(partners):
    barrier = pltpu.get_barrier_semaphore()
    for dev in partners:
        pl.semaphore_signal(barrier, inc=1, device_id={'cp': dev}, device_id_type=MESH)
    pl.semaphore_wait(barrier, len(partners))


def row_stats(do, o, lse, st):
    st[...] = jnp.zeros_like(st)
    tok = lax.broadcasted_iota(jnp.int32, (8, LANES), 0)
    lane = lax.broadcasted_iota(jnp.int32, (8, LANES), 1)
    for j in range(do.shape[0]):
        wide = jnp.concatenate([lse[j]] * 8, axis=1)
        st[j:j + 1, :] = jnp.sum(jnp.where((lane >> 4) == tok, wide, 0.0), axis=0, keepdims=True) * LOG2E
        prod = do[j].astype(F32) * o[j].astype(F32)
        st[8 + j:9 + j, :] = jnp.sum(prod.T, axis=0, keepdims=True)


def limits(doc, n_sub, sub_len, keys_local, lim, bnd):
    z, y, x, c = place()
    grp, lane = z * 4 + y, x * 2 + c
    n_pos = doc.shape[0] * LANES
    sub_start = n_pos - n_sub * sub_len
    period = 8 * keys_local

    def flat(pos):
        b = jnp.zeros_like(pos)
        for i in range(1, n_pos // period):
            b += jnp.where(pos >= i * period, 1, 0)
        return b * keys_local + jnp.clip(pos - b * period - lane * keys_local, 0, keys_local)

    sub = lax.broadcasted_iota(jnp.int32, (8, LANES), 0)
    tok = lax.broadcasted_iota(jnp.int32, (8, LANES), 1)
    docs = jnp.zeros((8, LANES), jnp.int32)
    for j in range(n_sub):
        row = doc[pl.ds((sub_start + j * sub_len) // LANES + grp // 2, 1), :]
        docs = jnp.where(sub == j, row, docs)
    docs = jnp.where(lax.rem(grp, 2) == 1, pltpu.roll(docs, 64, 1), docs)
    before = jnp.zeros((8, LANES), jnp.int32)
    for j in range(n_sub):
        head = docs[j:j + 1, 0:1]
        count = jnp.zeros((8, LANES), jnp.int32)
        for r in range(0, doc.shape[0], 8):
            count += jnp.where(doc[r:r + 8, :] < head, 1, 0)
        count = jnp.sum(jnp.sum(count.astype(F32), axis=0, keepdims=True), axis=1, keepdims=True)
        before = jnp.where(sub == j, count.astype(jnp.int32), before)
    base = sub_start + sub * sub_len + grp * 64
    pos = base + tok
    begin = jnp.where((tok > 0) & (docs != pltpu.roll(docs, 1, 1)), pos, before)
    for shift in (1, 2, 4, 8, 16, 32):
        begin = jnp.maximum(begin, jnp.where(tok >= shift, pltpu.roll(begin, shift, 1), 0))
    pick = jnp.where(
        lax.broadcasted_iota(jnp.int32, (LANES, 1024), 0) == lax.broadcasted_iota(jnp.int32, (LANES, 1024), 1) >> 4, 1.0, 0.0)
    for first, value in ((0, flat(begin)), (8, flat(pos + 1))):
        wide = jnp.dot(value.astype(F32), pick, precision=lax.Precision.HIGHEST, preferred_element_type=F32)
        for l in range(8):
            lim[l, first:first + 8, :] = wide[:, LANES * l:LANES * l + LANES].astype(jnp.int32)
    start = flat(before) & -16
    tiles = jnp.maximum((flat(base + 64) - start + (TK - 1)) // TK, 1)
    first = doc[pl.ds(sub_start // LANES, 1), :][:, 0:1]
    edge = lambda planes: doc[pl.ds((n_pos - planes * n_pos // 4 - 1) // LANES, 1), :][:, 127:LANES] >= first
    which = jnp.where(edge(1), jnp.where(edge(2), 2, 1), 0)
    bnd[...] = jnp.where(tok == 0, start, jnp.where(tok == 1, tiles, which))


def clear(zq, zk, zv):
    def rows(i, _):
        for r in range(4):
            at_ = pl.ds(pl.multiple_of((i * 4 + r) * 16, 16), 16)
            zk[at_, :] = jnp.zeros((16, LANES), F32)
            zv[at_, :] = jnp.zeros((16, LANES), F32)
        return 0

    lax.fori_loop(0, zk.shape[0] // 64, rows, 0)

    def block(i, _):
        zq[i // 8, lax.rem(i, 8)] = jnp.zeros((LANES, LANES), F32)
        return 0

    lax.fori_loop(0, zq.shape[0] * 8, block, 0)


def gather_body(sub_len, q, do, o, lse, doc, k, v, qg, dg, sg, kg, vg, lim, bnd, zq, zk, zv, st, ov, lv, cv, lsem, ssem, rsem):
    z, y, x, c = place()
    xu, xd, sib = at(z, y, up(x), c), at(z, y, down(x), c), at(z, y, x, 1 - c)
    yu, yd = at(z, up(y), x, c), at(z, down(y), x, c)
    zu, zd = at(up(z), y, x, c), at(down(z), y, x, c)
    lane = lambda xx: xx * 2 + c
    own = lane(x)
    loads = []
    for i, (src, dst) in enumerate((
            (k, kg.at[z, y]), (v, vg.at[z, y]), (q, qg.at[:, own]), (do, dg.at[:, own]), (o, ov), (lse, lv), (doc, cv))):
        loads.append(pltpu.make_async_copy(src, dst, lsem.at[i]))
        loads[i].start()
    greet([xu, xd, sib, yu, yd, zu, zd])
    w = Wire(ssem, rsem)
    ha, hb = slice(0, 3), slice(3, 6)
    pairs = (qg, dg)
    k, v = kg.at[z, y], vg.at[z, y]
    ru_a, rd_b, ru_b, rd_a = [], [], [], []
    loads[0].wait()
    k_u = w.send(k, k, yu)
    k_d = w.send(k, k, yd)
    loads[1].wait()
    v_u = w.send(v, v, zu)
    v_d = w.send(v, v, zd)
    for i, g in enumerate(pairs):
        loads[2 + i].wait()
        ru_a.append(w.send(g.at[ha, own], g.at[ha, own], xu))
        rd_b.append(w.send(g.at[hb, own], g.at[hb, own], xd))
    for g in pairs:
        ru_b.append(w.send(g.at[hb, own], g.at[hb, own], xu))
        rd_a.append(w.send(g.at[ha, own], g.at[ha, own], xd))
    sibs = [w.send(g.at[:, own], g.at[:, own], sib) for g in pairs]
    kz, vy = {}, {}
    kz['u', 0] = w.send(k, k, zu)
    kz['d', 0] = w.send(k, k, zd)
    vy['u', 0] = w.send(v, v, yu)
    vy['d', 0] = w.send(v, v, yd)
    for cp in loads[4:]:
        cp.wait()
    row_stats(dg.at[:, own], ov, lv, st)
    sg[own] = st[...]
    limits(cv, qg.shape[0], sub_len, kg.shape[2], lim, bnd)
    su = w.send(st, sg.at[own], xu)
    sd = w.send(st, sg.at[own], xd)
    sibs.append(w.send(st, sg.at[own], sib))
    lo_rows, hi_rows = pl.ds(0, 160), pl.ds(160, 144)
    clear(zq, zk, zv)
    k_u.wait_recv()
    kf_a = w.send(kg.at[z, down(y), lo_rows], kg.at[z, down(y), lo_rows], yu)
    k_d.wait_recv()
    kf_b = w.send(kg.at[z, up(y), hi_rows], kg.at[z, up(y), hi_rows], yd)
    v_u.wait_recv()
    vf_a = w.send(vg.at[down(z), y, lo_rows], vg.at[down(z), y, lo_rows], zu)
    v_d.wait_recv()
    vf_b = w.send(vg.at[up(z), y, hi_rows], vg.at[up(z), y, hi_rows], zd)
    for r, yy, zz in ((3, down(y), down(z)), (1, up(y), up(z))):
        for name, dev in (('u', zu), ('d', zd)):
            kz[name, r] = w.send(kg.at[z, yy], kg.at[z, yy], dev)
        for name, dev in (('u', yu), ('d', yd)):
            vy[name, r] = w.send(vg.at[zz, y], vg.at[zz, y], dev)
    kf_a.wait_recv()
    kf_b.wait_recv()
    for name, dev in (('u', zu), ('d', zd)):
        kz[name, 2] = w.send(kg.at[z, far(y)], kg.at[z, far(y)], dev)
    vf_a.wait_recv()
    vf_b.wait_recv()
    for name, dev in (('u', yu), ('d', yd)):
        vy[name, 2] = w.send(vg.at[far(z), y], vg.at[far(z), y], dev)
    ld, lu, lf = lane(down(x)), lane(up(x)), lane(far(x))
    fu, fd = [], []
    for i, g in enumerate(pairs):
        ru_a[i].wait_recv()
        fu.append(w.send(g.at[ha, ld], g.at[ha, ld], xu))
        rd_b[i].wait_recv()
        fd.append(w.send(g.at[hb, lu], g.at[hb, lu], xd))
    su.wait_recv()
    sf = w.send(sg.at[ld], sg.at[ld], xu)
    sd.wait_recv()
    for i, g in enumerate(pairs):
        sibs.append(w.send(g.at[ha, ld], g.at[ha, ld], sib))
        sibs.append(w.send(g.at[hb, lu], g.at[hb, lu], sib))
    sibs.append(w.send(sg.at[ld], sg.at[ld], sib))
    sibs.append(w.send(sg.at[lu], sg.at[lu], sib))
    slot = lambda r, v_: lax.rem(v_ + r, 4)
    kzf, vyf = [], []
    for r in (0, 3, 1, 2):
        if r == 2:
            for i, g in enumerate(pairs):
                ru_b[i].wait_recv()
                sibs.append(w.send(g.at[hb, ld], g.at[hb, ld], sib))
                rd_a[i].wait_recv()
                sibs.append(w.send(g.at[ha, lu], g.at[ha, lu], sib))
        yy, zz = slot(r, y), slot(r, z)
        kz['u', r].wait_recv()
        if r in (0, 1):
            kzf.append(w.send(kg.at[down(z), yy], kg.at[down(z), yy], zu))
        kz['d', r].wait_recv()
        if r in (2, 3):
            kzf.append(w.send(kg.at[up(z), yy], kg.at[up(z), yy], zd))
        vy['u', r].wait_recv()
        if r in (0, 1):
            vyf.append(w.send(vg.at[zz, down(y)], vg.at[zz, down(y)], yu))
        vy['d', r].wait_recv()
        if r in (2, 3):
            vyf.append(w.send(vg.at[zz, up(y)], vg.at[zz, up(y)], yd))
    sf.wait_recv()
    sibs.append(w.send(sg.at[lf], sg.at[lf], sib))
    for i, g in enumerate(pairs):
        fu[i].wait_recv()
        sibs.append(w.send(g.at[ha, lf], g.at[ha, lf], sib))
        fd[i].wait_recv()
        sibs.append(w.send(g.at[hb, lf], g.at[hb, lf], sib))
    for cp in kzf + vyf + sibs:
        cp.wait_recv()
    w.finish()


def gather(sub_len, q, do, o, lse, doc, k, v):
    n_sub = q.shape[0]
    vm = pl.BlockSpec(memory_space=pltpu.VMEM)
    return pl.pallas_call(
        functools.partial(gather_body, sub_len),
        in_specs=[pl.BlockSpec(memory_space=pltpu.HBM)] * 7,
        out_specs=[vm] * 10,
        out_shape=[
            jax.ShapeDtypeStruct((n_sub, 8, LANES, LANES), BF16),
            jax.ShapeDtypeStruct((n_sub, 8, LANES, LANES), BF16),
            jax.ShapeDtypeStruct((8, 16, LANES), F32),
            jax.ShapeDtypeStruct((4, 4) + k.shape, BF16),
            jax.ShapeDtypeStruct((4, 4) + k.shape, BF16),
            jax.ShapeDtypeStruct((8, 16, LANES), jnp.int32),
            jax.ShapeDtypeStruct((8, LANES), jnp.int32),
            jax.ShapeDtypeStruct((n_sub, 8, LANES, LANES), F32),
            jax.ShapeDtypeStruct((16 * k.shape[0], LANES), F32),
            jax.ShapeDtypeStruct((16 * k.shape[0], LANES), F32),
        ],
        scratch_shapes=[
            pltpu.VMEM((16, LANES), F32), pltpu.VMEM(o.shape, BF16), pltpu.VMEM(lse.shape, F32), pltpu.VMEM(doc.shape, jnp.int32),
            pltpu.SemaphoreType.DMA((7,)), pltpu.SemaphoreType.DMA((80,)), pltpu.SemaphoreType.DMA((80,))],
        compiler_params=pltpu.CompilerParams(collective_id=0, has_side_effects=True, vmem_limit_bytes=8 * 2**20),
        name='gather',
    )(*[pltpu.with_memory_space_constraint(a, pltpu.HBM) for a in (q, do, o, lse, doc, k, v)])


def attend_body(scale, bnd, kg, vg, q, do, st, lim, zq, zk, zv, dq, dk, dv, which, p0, d0, p1, d1):
    n_keys, n_sub, n_lane = kg.shape[0], q.shape[0], q.shape[1]

    p1[...] = jnp.zeros_like(p1)
    d1[...] = jnp.zeros_like(d1)
    which[0] = bnd[0, 2]
    total = bnd[0, 1]
    for j in range(1, n_sub):
        total = total + bnd[j, 1]

    def tile_of(j, i):
        nominal = bnd[j, 0] + i * TK
        return nominal, pl.multiple_of(jnp.minimum(nominal, n_keys - TK), 16)

    def front(j, i, pr, dr):
        nominal, first = tile_of(j, i)
        rows = pl.ds(first, TK)
        kt, vt = kg[rows, :], vg[rows, :]
        index = lax.broadcasted_iota(jnp.int32, (TK, LANES), 0) + first
        for m in range(n_lane // 2):
            qc = q[j, 2 * m:2 * m + 2].reshape(256, LANES)
            dc = do[j, 2 * m:2 * m + 2].reshape(256, LANES)
            s = lax.dot_general(kt, qc, (((1,), (1,)), ((), ())), preferred_element_type=F32)
            dp = lax.dot_general(vt, dc, (((1,), (1,)), ((), ())), preferred_element_type=F32)
            for h in range(2):
                l = 2 * m + h
                cols = slice(LANES * h, LANES * h + LANES)
                lse, delta = st[l, pl.ds(j, 1), :], st[l, pl.ds(j + 8, 1), :]
                low, high = lim[l, pl.ds(j, 1), :], lim[l, pl.ds(j + 8, 1), :]
                e = jnp.exp2(s[:, cols] * (scale * LOG2E) - lse)
                p = jnp.where((index >= jnp.maximum(low, nominal)) & (index < high), e, 0.0)
                pr[l] = p.astype(BF16)
                dr[l] = (p * (dp[:, cols] - delta)).astype(BF16)

    def back(j, i, pr, dr):
        rows = pl.ds(tile_of(j, i)[1], TK)
        ktt = kg[rows, :].T
        pa = jnp.concatenate([pr[l] for l in range(n_lane)], axis=1)
        da = jnp.concatenate([dr[l] for l in range(n_lane)], axis=1)
        dv[rows, :] += jnp.dot(pa, do[j].reshape(n_lane * LANES, LANES), preferred_element_type=F32)
        dk[rows, :] += jnp.dot(da, q[j].reshape(n_lane * LANES, LANES), preferred_element_type=F32)
        for m in range(n_lane // 2):
            t = jnp.dot(ktt, da[:, 256 * m:256 * m + 256], preferred_element_type=F32)
            dq[j, 2 * m] += t[:, :LANES]
            dq[j, 2 * m + 1] += t[:, LANES:]

    def after(j, i):
        turn = (i + 1 >= bnd[j, 1]) & (j < n_sub - 1)
        return jnp.where(turn, j + 1, j), jnp.where(turn, 0, i + 1)

    def two(_, at_):
        hj, hi, j, i = at_
        front(j, i, p0, d0)
        back(hj, hi, p1, d1)
        nj, ni = after(j, i)
        front(nj, ni, p1, d1)
        back(j, i, p0, d0)
        return (nj, ni) + after(nj, ni)

    zero = jnp.int32(0)
    lax.fori_loop(0, (total + 2) // 2, two, (zero, zero, zero, zero))


def attend(bnd, kg, vg, q, do, st, lim, zq, zk, zv):
    n_lane = q.shape[1]
    vm = pl.BlockSpec(memory_space=pltpu.VMEM)
    return pl.pallas_call(
        functools.partial(attend_body, LANES ** -0.5),
        in_specs=[pl.BlockSpec(memory_space=pltpu.SMEM)] + [vm] * 9,
        out_specs=[vm] * 3 + [pl.BlockSpec(memory_space=pltpu.SMEM)],
        out_shape=[jax.ShapeDtypeStruct(q.shape, F32), jax.ShapeDtypeStruct(kg.shape, F32),
                   jax.ShapeDtypeStruct(kg.shape, F32), jax.ShapeDtypeStruct((1,), jnp.int32)],
        input_output_aliases={7: 0, 8: 1, 9: 2},
        scratch_shapes=[pltpu.VMEM((n_lane, TK, LANES), BF16)] * 4,
        compiler_params=pltpu.CompilerParams(vmem_limit_bytes=16 * 2**20),
        name='attend',
    )(bnd, kg, vg, q, do, st, lim, zq, zk, zv)


class Split:
    def __init__(self, planes, keys):
        self.planes, self.keys, self.parts = planes, keys, 4 // planes
        self.rows = -(-keys // self.parts // 16) * 16 if planes == 1 else keys // self.parts
        self.low = self.rows // 2 if self.rows % 16 == 0 else self.rows // 16 * 8
        self.last = keys - self.rows
        self.half = {4: (2, keys, LANES), 2: (keys, LANES), 1: (2 * self.rows, LANES)}[planes]

    def slot(self, z):
        if self.planes == 4:
            return z, 0
        if self.planes == 2:
            return jnp.where(lax.rem(z, 3) == 0, 3, 2), jnp.where(z < 2, self.rows, 0)
        return 3, jnp.minimum(lax.rem(z + 1, 4) * self.rows, self.last)

    def rows_at(self, first):
        return pl.ds(first if isinstance(first, int) else pl.multiple_of(first, 8), self.rows)

    def keys_of(self, dk, z, ys):
        owner, first = self.slot(z)
        return dk.at[owner, ys, self.rows_at(first)]

    def values_of(self, dv, y, h):
        if self.planes == 4:
            return dv.at[pl.ds(2 * h, 2), y]
        if self.planes == 2:
            return dv.at[2 + h, y]
        return dv.at[3, y, pl.ds(h * (self.keys - 2 * self.rows), 2 * self.rows)]

    def value_slot(self, vs, z):
        owner, first = self.slot(z)
        if self.planes == 4:
            return vs.at[z // 2, lax.rem(z, 2)]
        if self.planes == 2:
            return vs.at[owner - 2, self.rows_at(first)]
        h = jnp.where(first >= 2 * self.rows, 1, 0)
        return vs.at[h, self.rows_at(first - h * (self.keys - 2 * self.rows))]

    def shares(self):
        if self.planes == 4:
            return []
        if self.planes == 2:
            return [(3, 1, 0), (2, 1, 1)]
        return [(3, h, (3 + h) % 4) for h in (1, 2, 3)]


class Ring:
    def __init__(self, w, place_, dev_up, dev_down, block, via, got):
        self.w, self.p, self.up, self.dn = w, place_, dev_up, dev_down
        self.block, self.via, self.got = block, via, got

    def first(self):
        w, p = self.w, self.p
        self.fu = w.send(self.block(far(p), 0), self.via(0), self.up)
        self.fd = w.send(self.block(far(p), 1), self.via(1), self.dn)

    def direct_up(self):
        self.du = self.w.send(self.block(up(self.p), 1), self.got(0, 1), self.up)

    def direct_down(self):
        self.dd = self.w.send(self.block(down(self.p), 0), self.got(1, 0), self.dn)

    def start(self):
        self.first()
        self.direct_up()
        self.direct_down()

    def middle(self):
        w, p = self.w, self.p
        self.fu.wait_recv()
        add(self.via(0), self.block(up(p), 0))
        self.mu = w.send(self.via(0), self.got(0, 0), self.up)
        self.fd.wait_recv()
        add(self.via(1), self.block(down(p), 1))
        self.md = w.send(self.via(1), self.got(1, 1), self.dn)

    def wait(self):
        for cp in (self.du, self.dd, self.mu, self.md):
            cp.wait_recv()


def add(dst, src):
    dst[...] = dst[...] + src[...]


def scatter_body(scale, sp, dq, dk, dv, oq, ok, ov, sq, sv, sg, k1v, k1g, ks, k2v, k2g, kr, v1v, v1g, vs, v2v, v2g, vr, ssem, rsem):
    z, y, x, c = place()
    xu, xd, sib = at(z, y, up(x), c), at(z, y, down(x), c), at(z, y, x, 1 - c)
    yu, yd = at(z, up(y), x, c), at(z, down(y), x, c)
    zu, zd = at(up(z), y, x, c), at(down(z), y, x, c)
    greet([xu, xd, sib, yu, yd, zu, zd] + ([at(far(z), y, x, c)] if sp.planes == 1 else []))
    w = Wire(ssem, rsem)
    n_sub = dq.shape[0]
    hn = n_sub // 2
    order = (far(x), up(x), down(x), x)
    cross = [w.send(dq.at[:, xx * 2 + 1 - c], sq.at[xx], sib) for xx in order]
    hy = (pl.ds(0, 2), pl.ds(2, 2))
    kone = Ring(w, z, zu, zd, lambda b, h: sp.keys_of(dk, b, hy[h]), lambda h: k1v.at[h], lambda s, h: k1g.at[s, hy[h]])
    vone = Ring(w, y, yu, yd, lambda b, h: sp.values_of(dv, b, h), lambda h: v1v.at[h], lambda s, h: v1g.at[s, h])
    kone.start()
    vone.start()
    hj = (pl.ds(0, hn), pl.ds(hn, n_sub - hn))
    qring = Ring(w, x, xu, xd, lambda b, h: sq.at[b, hj[h]], lambda h: sv.at[h], lambda s, h: sg.at[s, hj[h]])
    for cp, xx, then in zip(cross, order, (qring.first, qring.direct_up, qring.direct_down, None)):
        cp.wait_recv()
        for j in range(n_sub):
            sq[xx, j] = sq[xx, j] + dq[j, xx * 2 + c]
        if then is not None:
            then()
    kone.middle()
    vone.middle()
    qring.middle()
    nr = (sp.low, sp.rows - sp.low)
    hr = (pl.ds(0, nr[0]), pl.ds(nr[0], nr[1]))
    ktwo = Ring(w, y, yu, yd, lambda b, h: ks.at[b, hr[h]], lambda h: k2v.at[h, pl.ds(0, nr[h])], lambda s, h: k2g.at[s, hr[h]])
    vtwo = Ring(w, z, zu, zd, lambda b, h: sp.value_slot(vs, b).at[hr[h]], lambda h: v2v.at[h, pl.ds(0, nr[h])],
                lambda s, h: v2g.at[s, hr[h]])
    kone.wait()
    for b in range(4):
        ks[b] = sp.keys_of(dk, z, b)[...] + k1g[0, b] + k1g[1, b]
    ktwo.start()
    vone.wait()
    for h in range(2):
        vs[h] = sp.values_of(dv, y, h)[...] + v1g[0, h] + v1g[1, h]
    vtwo.start()
    ktwo.middle()
    vtwo.middle()
    ktwo.wait()
    kr[0] = (ks[y] + k2g[0] + k2g[1]) * scale
    vtwo.wait()
    vr[0] = sp.value_slot(vs, z)[...] + v2g[0] + v2g[1]
    home = []
    for owner, h, taker in sp.shares():
        for buf, out in ((kr, ok), (vr, ov)):
            cp = w.copy(buf.at[0], buf.at[h], at(owner, y, x, c))
            home.append((owner, h, taker, buf, out, cp))
            pl.when(z == taker)(cp.start)
    qring.wait()
    for j in range(n_sub):
        oq[j] = ((sq[x, j] + sg[0, j] + sg[1, j]).T * scale).astype(BF16)
    if sp.planes == 4:
        ok[...] = kr[0]
        ov[...] = vr[0]
    else:
        @pl.when(z < 4 - sp.planes)
        def _():
            ok[...] = jnp.zeros_like(ok)
            ov[...] = jnp.zeros_like(ov)

        @pl.when(z >= 4 - sp.planes)
        def _():
            ok[0:sp.rows, :] = kr[0]
            ov[0:sp.rows, :] = vr[0]

        for owner, h, taker, buf, out, cp in home:
            first = min(h * sp.rows, sp.last)

            @pl.when(z == owner)
            def _():
                cp.wait_recv()
                out[first:first + sp.rows, :] = buf[h]

            pl.when(z == taker)(cp.wait_send)
    w.finish()


def scatter(planes, dq, dk, dv):
    n_sub = dq.shape[0]
    sp = Split(planes, dk.shape[2])
    rows = sp.rows
    vm = pl.BlockSpec(memory_space=pltpu.VMEM)
    two = [
        pltpu.VMEM((2, sp.low + sp.low % 16, LANES), F32),
        pltpu.VMEM((2, rows, LANES), F32),
        pltpu.VMEM((sp.parts, rows, LANES), F32),
    ]
    return pl.pallas_call(
        functools.partial(scatter_body, LANES ** -0.5, sp),
        in_specs=[vm] * 3,
        out_specs=[vm] * 3,
        out_shape=[
            jax.ShapeDtypeStruct((n_sub, LANES, LANES), BF16),
            jax.ShapeDtypeStruct((sp.keys, LANES), F32),
            jax.ShapeDtypeStruct((sp.keys, LANES), F32),
        ],
        scratch_shapes=[
            pltpu.VMEM((4, n_sub, LANES, LANES), F32),
            pltpu.VMEM((2, n_sub // 2, LANES, LANES), F32),
            pltpu.VMEM((2, n_sub, LANES, LANES), F32),
            pltpu.VMEM((2, 2, rows, LANES), F32), pltpu.VMEM((2, 4, rows, LANES), F32), pltpu.VMEM((4, rows, LANES), F32), *two,
            pltpu.VMEM((2,) + sp.half, F32), pltpu.VMEM((2, 2) + sp.half, F32), pltpu.VMEM((2,) + sp.half, F32), *two,
            pltpu.SemaphoreType.DMA((44,)), pltpu.SemaphoreType.DMA((44,))],
        compiler_params=pltpu.CompilerParams(collective_id=planes, has_side_effects=True, vmem_limit_bytes=20 * 2**20),
        name='scatter',
    )(dq, dk, dv)


def solution(mesh):
    q_spec = P(None, 'cp', 'tp', None)
    lse_spec = P(None, 'cp', 'tp')
    kv_spec = P('cp', 'tp', None)

    def local_backward(query, out_act, out_grad, row_lse, key_act, value_act, doc_ids):
        n_sub, local_len, n_heads, head_dim = query.shape
        keys_local = key_act.shape[0]
        rows = local_len * n_heads
        q = query.reshape(n_sub, rows, head_dim)
        do = out_grad.reshape(n_sub, rows, head_dim)
        o = out_act.reshape(n_sub, rows, head_dim)
        doc = doc_ids.reshape(-1, LANES)
        k, v = key_act.reshape(keys_local, head_dim), value_act.reshape(keys_local, head_dim)
        qg, dg, sg, kg, vg, lim, bnd, zq, zk, zv = gather(local_len * LANES, q, do, o, row_lse, doc, k, v)
        flat = (16 * keys_local, head_dim)
        dq, dk, dv, which = attend(bnd, kg.reshape(flat), vg.reshape(flat), qg, dg, sg, lim, zq, zk, zv)
        blocks = (4, 4, keys_local, head_dim)
        oq, ok, ov = lax.switch(which[0], [functools.partial(scatter, n) for n in (1, 2, 4)], dq, dk.reshape(blocks), dv.reshape(blocks))
        return (oq.reshape(query.shape), ok.reshape(keys_local, 1, head_dim), ov.reshape(keys_local, 1, head_dim))

    return jax.shard_map(local_backward, mesh=mesh, in_specs=(q_spec, q_spec, q_spec, lse_spec, kv_spec, kv_spec, P()), out_specs=(q_spec, kv_spec, kv_spec), check_vma=False)
```

profile of v0, /device:TPU:0, one launch (start us, length us, event | category | flops | bytes accessed | tf_op | source)
XLA Modules:
  0.0 59.3 jit_solution(7552451970161933353)
XLA Ops:
  0.6 25.0 %gather.1 = (bf16[6,8,128,128]{3,2,1,0:T(8,128)(2,1)S(1)}, bf16[6,8,128,128]{3,2,1,0:T(8,128)(2,1)S(1)}, f32[8,16,128]{2,1,0:T(8,128)S(1)}, bf16[4,4,304,128]{3,...) custom-call(bf16[6,128,128]{2,1,0:T(8,128)(2,1)} %bitcast.22, ...), custom_call_target="tpu_custom_call" | custom-call | tf_op jit(solution)/shard_map/gather/pallas_call | solution.py:262
  25.7 8.6 %attend.1 = (f32[6,8,128,128]{3,2,1,0:T(8,128)S(1)}, f32[4864,128]{1,0:T(8,128)S(1)}, f32[4864,128]{1,0:T(8,128)S(1)}, s32[1]{0:T(128)}) custom-call(s32[8,128]{1,0:T(8,128)S(1)} %get-tuple-element.65.bnd, bf16[4864,128]{1,0:T(8,128)(2,1)S(1)} %bitcast.14, ...), custom_call_target="tpu_custom_call", output_to_operand_aliasing={{0}: (7, {}), {1}: (8, {}), {2}: (9, {})} | custom-call | tf_op jit(solution)/shard_map/attend/pallas_call | solution.py:352
  34.9 22.3 %conditional.1 = ((bf16[6,128,128]{2,1,0:T(8,128)(2,1)S(1)}, f32[304,128]{1,0:T(8,128)S(1)}, f32[304,128]{1,0:T(8,128)S(1)})) conditional(s32[]{:T(128)} %bitcast.8, (f32[6,8,128,128]{3,2,1,0:T(8,128)S(1)}, f32[4,4,304,128]{3,2,1,0:T(8,128)S(1)}, f32[4,4,304,128]{3,2,1,0:T(8,128)S(1)}) %tuple.44, (f32[6,8,128,128]{3,2,1,0:T(8,128)S(1)}, ...), branch_computations={%region_0.0_spmd, %region_1.0_spmd, %region_2.0_spmd} | conditional | bytes 8 | solution.py:580
  34.9 22.3 %scatter.3 = (bf16[6,128,128]{2,1,0:T(8,128)(2,1)S(1)}, f32[304,128]{1,0:T(8,128)S(1)}, f32[304,128]{1,0:T(8,128)S(1)}) custom-call(f32[6,8,128,128]{3,2,1,0:T(8,128)S(1)} %get-tuple-element.30.dq, f32[4,4,304,128]{3,2,1,0:T(8,128)S(1)} %get-tuple-element.31.dk, f32[4,4,304,128]{3,2,1,0:T(8,128)S(1)} %get-tuple-element.32.dv), custom_call_target="tpu_custom_call" | custom-call | tf_op jit(solution)/shard_map/cond/branch_0_fun/scatter/pallas_call | solution.py:541
  57.3 0.7 %copy.28 = bf16[6,8,16,128]{3,2,1,0:T(8,128)(2,1)} copy(bf16[6,8,16,128]{3,2,1,0:T(8,128)(2,1)S(1)} %bitcast.25) | data formatting | bytes 393216
  57.9 0.7 %copy.29 = f32[304,1,128]{2,1,0:T(1,128)} copy(f32[304,1,128]{2,1,0:T(1,128)S(1)} %bitcast.27) | data formatting | bytes 311296
  58.6 0.7 %copy.30 = f32[304,1,128]{2,1,0:T(1,128)} copy(f32[304,1,128]{2,1,0:T(1,128)S(1)} %bitcast.28) | data formatting | bytes 311296
where the time goes:
time: 59.6 us; the launch traced here: 59.3 us
  Pallas kernels  55.9 us (94%)
  local copies, waits for them, and re-layouts  2.01 us (3%)
  between operations  1.31 us (2%)
    pallas_call x1, Pallas kernels, gather(): pl.pallas_call(functools.partial(gather_body, sub_len), in_specs=[pl.Bloc...  25 us
    pallas_call x1, Pallas kernels, scatter(): pl.pallas_call(functools.partial(scatter_body, LANES ** (-0.5), sp), in_s...  22.3 us
    pallas_call x1, Pallas kernels, attend(): pl.pallas_call(functools.partial(attend_body, LANES ** (-0.5)), in_specs=...  8.59 us
    unnamed x3, local copies, waits for them, and re-layouts  2.01 us

commit v1 on v0

--- a/solution.py
+++ b/solution.py
@@ -115,7 +115,7 @@
         for l in range(8):
             lim[l, first:first + 8, :] = wide[:, LANES * l:LANES * l + LANES].astype(jnp.int32)
     start = flat(before) & -16
-    tiles = jnp.maximum((flat(base + 64) - start + (TK - 1)) // TK, 1)
+    tiles = jnp.maximum((flat(base + 64) - start + (TK - 1)) // TK, jnp.where(sub == 0, 1, 0))
     first = doc[pl.ds(sub_start // LANES, 1), :][:, 0:1]
     edge = lambda planes: doc[pl.ds((n_pos - planes * n_pos // 4 - 1) // LANES, 1), :][:, 127:LANES] >= first
     which = jnp.where(edge(1), jnp.where(edge(2), 2, 1), 0)
@@ -286,8 +286,6 @@
 def attend_body(scale, bnd, kg, vg, q, do, st, lim, zq, zk, zv, dq, dk, dv, which, p0, d0, p1, d1):
     n_keys, n_sub, n_lane = kg.shape[0], q.shape[0], q.shape[1]
 
-    p1[...] = jnp.zeros_like(p1)
-    d1[...] = jnp.zeros_like(d1)
     which[0] = bnd[0, 2]
     total = bnd[0, 1]
     for j in range(1, n_sub):
@@ -302,7 +300,8 @@
         rows = pl.ds(first, TK)
         kt, vt = kg[rows, :], vg[rows, :]
         index = lax.broadcasted_iota(jnp.int32, (TK, LANES), 0) + first
-        for m in range(n_lane // 2):
+
+        def chunk(m):
             qc = q[j, 2 * m:2 * m + 2].reshape(256, LANES)
             dc = do[j, 2 * m:2 * m + 2].reshape(256, LANES)
             s = lax.dot_general(kt, qc, (((1,), (1,)), ((), ())), preferred_element_type=F32)
@@ -317,33 +316,64 @@
                 pr[l] = p.astype(BF16)
                 dr[l] = (p * (dp[:, cols] - delta)).astype(BF16)
 
+        return [functools.partial(chunk, m) for m in range(n_lane // 2)]
+
     def back(j, i, pr, dr):
         rows = pl.ds(tile_of(j, i)[1], TK)
-        ktt = kg[rows, :].T
-        pa = jnp.concatenate([pr[l] for l in range(n_lane)], axis=1)
-        da = jnp.concatenate([dr[l] for l in range(n_lane)], axis=1)
-        dv[rows, :] += jnp.dot(pa, do[j].reshape(n_lane * LANES, LANES), preferred_element_type=F32)
-        dk[rows, :] += jnp.dot(da, q[j].reshape(n_lane * LANES, LANES), preferred_element_type=F32)
-        for m in range(n_lane // 2):
-            t = jnp.dot(ktt, da[:, 256 * m:256 * m + 256], preferred_element_type=F32)
-            dq[j, 2 * m] += t[:, :LANES]
-            dq[j, 2 * m + 1] += t[:, LANES:]
+        wide = lambda ref, ls: jnp.concatenate([ref[l] for l in ls], axis=1)
+
+        def values():
+            dv[rows, :] += jnp.dot(wide(pr, range(n_lane)), do[j].reshape(n_lane * LANES, LANES), preferred_element_type=F32)
+
+        def keys():
+            t = lax.dot_general(q[j].reshape(n_lane * LANES, LANES).T, wide(dr, range(n_lane)), (((1,), (1,)), ((), ())), preferred_element_type=F32)
+            dk[rows, :] += t.T
+
+        def queries():
+            ktt = kg[rows, :].T
+            for m in range(n_lane // 2):
+                t = jnp.dot(ktt, wide(dr, (2 * m, 2 * m + 1)), preferred_element_type=F32)
+                dq[j, 2 * m] += t[:, :LANES]
+                dq[j, 2 * m + 1] += t[:, LANES:]
+
+        return [values, keys, queries]
+
+    def do_all(*parts):
+        for part in parts:
+            part()
+
+    def beyond(j):
+        nxt = n_sub - 1
+        for jj in reversed(range(n_sub - 1)):
+            nxt = jnp.where((jj > j) & (bnd[jj, 1] > 0), jj, nxt)
+        return nxt
 
     def after(j, i):
-        turn = (i + 1 >= bnd[j, 1]) & (j < n_sub - 1)
-        return jnp.where(turn, j + 1, j), jnp.where(turn, 0, i + 1)
-
-    def two(_, at_):
-        hj, hi, j, i = at_
-        front(j, i, p0, d0)
-        back(hj, hi, p1, d1)
-        nj, ni = after(j, i)
-        front(nj, ni, p1, d1)
-        back(j, i, p0, d0)
-        return (nj, ni) + after(nj, ni)
-
-    zero = jnp.int32(0)
-    lax.fori_loop(0, (total + 2) // 2, two, (zero, zero, zero, zero))
+        turn = i + 1 >= bnd[j, 1]
+        return jnp.where(turn, beyond(j), j), jnp.where(turn, 0, i + 1)
+
+    def step(now, have, want):
+        nxt = after(*now)
+        b, f = back(*now, *have), front(*nxt, *want)
+        do_all(b[0], f[0], f[1], b[1], f[2], f[3], b[2])
+        return nxt
+
+    def four(_, now):
+        for _ in range(2):
+            now = step(step(now, (p0, d0), (p1, d1)), (p1, d1), (p0, d0))
+        return now
+
+    def one(_, now):
+        nxt = after(*now)
+        do_all(*back(*now, p0, d0), *front(*nxt, p0, d0))
+        return nxt
+
+    first = (beyond(jnp.int32(-1)), jnp.int32(0))
+    do_all(*front(*first, p0, d0))
+    more = total - 1
+    now = lax.fori_loop(0, more // 4, four, first)
+    now = lax.fori_loop(0, lax.rem(more, 4), one, now)
+    do_all(*back(*now, p0, d0))
 
 
 def attend(bnd, kg, vg, q, do, st, lim, zq, zk, zv):
@@ -413,10 +443,11 @@
         self.w, self.p, self.up, self.dn = w, place_, dev_up, dev_down
         self.block, self.via, self.got = block, via, got
 
-    def first(self):
-        w, p = self.w, self.p
-        self.fu = w.send(self.block(far(p), 0), self.via(0), self.up)
-        self.fd = w.send(self.block(far(p), 1), self.via(1), self.dn)
+    def first_up(self):
+        self.fu = self.w.send(self.block(far(self.p), 0), self.via(0), self.up)
+
+    def first_down(self):
+        self.fd = self.w.send(self.block(far(self.p), 1), self.via(1), self.dn)
 
     def direct_up(self):
         self.du = self.w.send(self.block(up(self.p), 1), self.got(0, 1), self.up)
@@ -425,7 +456,8 @@
         self.dd = self.w.send(self.block(down(self.p), 0), self.got(1, 0), self.dn)
 
     def start(self):
-        self.first()
+        self.first_up()
+        self.first_down()
         self.direct_up()
         self.direct_down()
 
@@ -456,8 +488,9 @@
     w = Wire(ssem, rsem)
     n_sub = dq.shape[0]
     hn = n_sub // 2
-    order = (far(x), up(x), down(x), x)
-    cross = [w.send(dq.at[:, xx * 2 + 1 - c], sq.at[xx], sib) for xx in order]
+    halves = (range(hn), range(hn, n_sub))
+    order = ((far(x), halves[0]), (far(x), halves[1]), (up(x), range(n_sub)), (down(x), range(n_sub)), (x, range(n_sub)))
+    cross = [w.send(dq.at[pl.ds(js[0], len(js)), xx * 2 + 1 - c], sq.at[xx, pl.ds(js[0], len(js))], sib) for xx, js in order]
     hy = (pl.ds(0, 2), pl.ds(2, 2))
     kone = Ring(w, z, zu, zd, lambda b, h: sp.keys_of(dk, b, hy[h]), lambda h: k1v.at[h], lambda s, h: k1g.at[s, hy[h]])
     vone = Ring(w, y, yu, yd, lambda b, h: sp.values_of(dv, b, h), lambda h: v1v.at[h], lambda s, h: v1g.at[s, h])
@@ -465,9 +498,10 @@
     vone.start()
     hj = (pl.ds(0, hn), pl.ds(hn, n_sub - hn))
     qring = Ring(w, x, xu, xd, lambda b, h: sq.at[b, hj[h]], lambda h: sv.at[h], lambda s, h: sg.at[s, hj[h]])
-    for cp, xx, then in zip(cross, order, (qring.first, qring.direct_up, qring.direct_down, None)):
+    steps = (qring.first_up, qring.first_down, qring.direct_up, qring.direct_down, None)
+    for cp, (xx, js), then in zip(cross, order, steps):
         cp.wait_recv()
-        for j in range(n_sub):
+        for j in js:
             sq[xx, j] = sq[xx, j] + dq[j, xx * 2 + c]
         if then is not None:
             then()
@@ -491,14 +525,18 @@
     vtwo.middle()
     ktwo.wait()
     kr[0] = (ks[y] + k2g[0] + k2g[1]) * scale
-    vtwo.wait()
-    vr[0] = sp.value_slot(vs, z)[...] + v2g[0] + v2g[1]
     home = []
-    for owner, h, taker in sp.shares():
-        for buf, out in ((kr, ok), (vr, ov)):
+
+    def go_home(buf, out):
+        for owner, h, taker in sp.shares():
             cp = w.copy(buf.at[0], buf.at[h], at(owner, y, x, c))
             home.append((owner, h, taker, buf, out, cp))
             pl.when(z == taker)(cp.start)
+
+    go_home(kr, ok)
+    vtwo.wait()
+    vr[0] = sp.value_slot(vs, z)[...] + v2g[0] + v2g[1]
+    go_home(vr, ov)
     qring.wait()
     for j in range(n_sub):
         oq[j] = ((sq[x, j] + sg[0, j] + sg[1, j]).T * scale).astype(BF16)
@@ -559,6 +597,25 @@
     )(dq, dk, dv)
 
 
+def store_body(a, b, c, oa, ob, oc, sem):
+    copies = [pltpu.make_async_copy(src, dst, sem.at[i]) for i, (src, dst) in enumerate(((a, oa), (b, ob), (c, oc)))]
+    for cp in copies:
+        cp.start()
+    for cp in copies:
+        cp.wait()
+
+
+def store(*arrays):
+    return pl.pallas_call(
+        store_body,
+        in_specs=[pl.BlockSpec(memory_space=pltpu.VMEM)] * 3,
+        out_specs=[pl.BlockSpec(memory_space=pltpu.HBM)] * 3,
+        out_shape=[jax.ShapeDtypeStruct(a.shape, a.dtype) for a in arrays],
+        scratch_shapes=[pltpu.SemaphoreType.DMA((3,))],
+        name='store',
+    )(*arrays)
+
+
 def solution(mesh):
     q_spec = P(None, 'cp', 'tp', None)
     lse_spec = P(None, 'cp', 'tp')
@@ -578,6 +635,7 @@
         dq, dk, dv, which = attend(bnd, kg.reshape(flat), vg.reshape(flat), qg, dg, sg, lim, zq, zk, zv)
         blocks = (4, 4, keys_local, head_dim)
         oq, ok, ov = lax.switch(which[0], [functools.partial(scatter, n) for n in (1, 2, 4)], dq, dk.reshape(blocks), dv.reshape(blocks))
+        oq, ok, ov = store(oq, ok, ov)
         return (oq.reshape(query.shape), ok.reshape(keys_local, 1, head_dim), ov.reshape(keys_local, 1, head_dim))
 
     return jax.shard_map(local_backward, mesh=mesh, in_specs=(q_spec, q_spec, q_spec, lse_spec, kv_spec, kv_spec, P()), out_specs=(q_spec, kv_spec, kv_spec), check_vma=False)

time: 59.6 us -> 57 us (0.956)
  local copies, waits for them, and re-layouts: 2.01 us -> 0 us
    pallas_call x1, Pallas kernels: 8.59 us -> 6.07 us  [attend(): pl.pallas_call(functools.partial(attend_body, LANES ** (-0.5)), in_specs=...]
    unnamed x3 -> x0, local copies, waits for them, and re-layouts: 2.01 us -> none
    pallas_call x0 -> x1, Pallas kernels: none -> 1.72 us  [store(): pl.pallas_call(store_body, in_specs=[pl.BlockSpec(memory_space=pltpu.VMEM...]
where the time goes in v1:
time: 57 us; the launch traced here: 56.7 us
  Pallas kernels  55.4 us (97%)
  between operations  1.3 us (2%)
    pallas_call x1, Pallas kernels, gather(): pl.pallas_call(functools.partial(gather_body, sub_len), in_specs=[pl.Bloc...  25 us
    pallas_call x1, Pallas kernels, scatter(): pl.pallas_call(functools.partial(scatter_body, LANES ** (-0.5), sp), in_s...  22.6 us
    pallas_call x1, Pallas kernels, attend(): pl.pallas_call(functools.partial(attend_body, LANES ** (-0.5)), in_specs=...  6.07 us
    pallas_call x1, Pallas kernels, store(): pl.pallas_call(store_body, in_specs=[pl.BlockSpec(memory_space=pltpu.VMEM...  1.72 us

profile of v1, /device:TPU:0, one launch (start us, length us, event | category | flops | bytes accessed | tf_op | source)
XLA Modules:
  0.0 56.7 jit_solution(11308753354177185516)
XLA Ops:
  0.6 25.0 %gather.1 = (bf16[6,8,128,128]{3,2,1,0:T(8,128)(2,1)S(1)}, bf16[6,8,128,128]{3,2,1,0:T(8,128)(2,1)S(1)}, f32[8,16,128]{2,1,0:T(8,128)S(1)}, bf16[4,4,304,128]{3,...) custom-call(bf16[6,128,128]{2,1,0:T(8,128)(2,1)} %bitcast.26, ...), custom_call_target="tpu_custom_call" | custom-call | tf_op jit(solution)/shard_map/gather/pallas_call | solution.py:262
  25.7 6.1 %attend.1 = (f32[6,8,128,128]{3,2,1,0:T(8,128)S(1)}, f32[4864,128]{1,0:T(8,128)S(1)}, f32[4864,128]{1,0:T(8,128)S(1)}, s32[1]{0:T(128)}) custom-call(s32[8,128]{1,0:T(8,128)S(1)} %get-tuple-element.50.bnd, bf16[4864,128]{1,0:T(8,128)(2,1)S(1)} %bitcast.18, ...), custom_call_target="tpu_custom_call", output_to_operand_aliasing={{0}: (7, {}), {1}: (8, {}), {2}: (9, {})} | custom-call | tf_op jit(solution)/shard_map/attend/pallas_call | solution.py:382
  32.4 22.6 %conditional.1 = ((bf16[6,128,128]{2,1,0:T(8,128)(2,1)S(1)}, f32[304,128]{1,0:T(8,128)S(1)}, f32[304,128]{1,0:T(8,128)})) conditional(s32[]{:T(128)} %bitcast.8, (f32[6,8,128,128]{3,2,1,0:T(8,128)S(1)}, f32[4,4,304,128]{3,2,1,0:T(8,128)S(1)}, f32[4,4,304,128]{3,2,1,0:T(8,128)S(1)}) %tuple.29, (f32[6,8,128,128]{3,2,1,0:T(8,128)S(1)}, ...), branch_computations={%region_0.0_spmd, %region_1.0_spmd, %region_2.0_spmd} | conditional | bytes 8 | solution.py:637
  32.4 22.6 %scatter.3 = (bf16[6,128,128]{2,1,0:T(8,128)(2,1)S(1)}, f32[304,128]{1,0:T(8,128)S(1)}, f32[304,128]{1,0:T(8,128)}) custom-call(f32[6,8,128,128]{3,2,1,0:T(8,128)S(1)} %get-tuple-element.18.dq, f32[4,4,304,128]{3,2,1,0:T(8,128)S(1)} %get-tuple-element.19.dk, f32[4,4,304,128]{3,2,1,0:T(8,128)S(1)} %get-tuple-element.20.dv), custom_call_target="tpu_custom_call" | custom-call | tf_op jit(solution)/shard_map/cond/branch_0_fun/scatter/pallas_call | solution.py:579
  55.0 1.7 %store.1 = (bf16[6,128,128]{2,1,0:T(8,128)(2,1)}, f32[304,128]{1,0:T(8,128)}, f32[304,128]{1,0:T(8,128)}) custom-call(bf16[6,128,128]{2,1,0:T(8,128)(2,1)S(1)} %get-tuple-element.64.a, f32[304,128]{1,0:T(8,128)S(1)} %get-tuple-element.65.b, f32[304,128]{1,0:T(8,128)} %get-tuple-element.66.c), custom_call_target="tpu_custom_call" | custom-call | tf_op jit(solution)/shard_map/store/pallas_call | solution.py:609
